TPU v7x, 32 devices: a whole 2x2x4 slice. The times are simulated.
32 devices in a mesh: parts: 2 (over y), pix: 4 (over z), par: 4 (over x, core).
Axes of the slice: x: 2, y: 2, z: 4, core: 2. Of those that a mesh axis runs over, the one named last changes fastest.
Arguments:
- green_matrix: bfloat16 [4608, 16384], P('pix', 'par'), may hold values from -0.046875 to 0.046875
- observed: bfloat16 [64, 4608], P('parts', 'pix'), parts along dimension 0, may hold values from -1000 to 1000
Outputs:
- solution: float32 [64, 16384], P('parts', 'par'), parts along dimension 0
- residual: float32 [64, 4608], P('parts', 'pix'), parts along dimension 0
There are 2 independent parts, one for each index of `parts`. A program takes and returns all parts, laid end to end along the dimension named above; an argument that names none is the same for every part. Nothing has to cross between parts.
All inputs are finite; a program needn't handle non-finite values.
Results may differ from a plain program's by a relative error of at most 0.0038.
Values may be sent and summed in bfloat16 or wider, within the bound.
A program may use at most 64 MiB of HBM per device.

v0:
```python
import functools

import jax
import jax.numpy as jnp
from jax import lax
from jax.experimental import pallas as pl
from jax.experimental.pallas import tpu as pltpu
from jax.sharding import PartitionSpec as P

GRID = 128
ITERS = 5
LANES = 128
SUB = 2


def padded_2(block, sides, width):
    for axis, dim in sides:
        count = lax.axis_size(axis)
        forward = [(i, i + 1) for i in range(count - 1)]
        backward = [(target, source) for source, target in forward]
        low = lax.ppermute(
            lax.slice_in_dim(block, block.shape[dim] - width, None, axis=dim), axis, forward
        )
        high = lax.ppermute(lax.slice_in_dim(block, 0, width, axis=dim), axis, backward)
        block = jnp.concatenate([low, block, high], axis=dim)
    return block


def smooth(values):
    set_count = values.shape[0]
    grid_rows = values.shape[1] // GRID
    tiles = values.reshape(set_count, grid_rows, GRID)
    padded = padded_2(tiles, (("par", 1),), 1)
    padded = jnp.pad(padded, ((0, 0), (0, 0), (1, 1)))
    beside_all = (
        padded[:, 2:, 1:-1] + padded[:, :-2, 1:-1] + padded[:, 1:-1, 2:] + padded[:, 1:-1, :-2]
    )
    return (0.25 * (4.0 * tiles - beside_all)).reshape(set_count, grid_rows * GRID)


def forward(rounded, green_matrix):
    partial_value = lax.dot_general(
        rounded, green_matrix, (((1,), (1,)), ((), ())), preferred_element_type=jnp.float32
    )
    return lax.psum(partial_value, "par")


def curvatures(image, smoothed):
    local_image = jnp.sum(image * image, axis=1)
    local_smooth = jnp.sum(smoothed * smoothed, axis=1)
    image_sq = lax.psum(local_image, "pix")
    smooth_sq = lax.psum(local_smooth, "par")
    return image_sq + smooth_sq


def backward_sum(rounded, green_matrix):
    return lax.psum(jnp.dot(rounded, green_matrix, preferred_element_type=jnp.float32), "pix")


def column_squares(gradient):
    return lax.psum(jnp.sum(gradient * gradient, axis=1), "par")


def on_device(green_matrix, observed):
    set_count = observed.shape[0]
    tile_cells = green_matrix.shape[1]
    residual = observed.astype(jnp.float32)
    gradient = backward_sum(observed, green_matrix)
    grad_sq = column_squares(gradient)
    direction = gradient
    solution = jnp.zeros((set_count, tile_cells), jnp.float32)
    smooth_res = jnp.zeros((set_count, tile_cells), jnp.float32)
    for sweep in range(ITERS):
        rounded = direction.astype(jnp.bfloat16)
        image = forward(rounded, green_matrix)
        smoothed = smooth(lax.optimization_barrier(rounded).astype(jnp.float32))
        step_len = (grad_sq / curvatures(image, smoothed))[:, None]
        solution = solution + step_len * direction
        residual = residual - step_len * image
        smooth_res = smooth_res - step_len * smoothed
        if sweep + 1 < ITERS:
            gradient = backward_sum(residual.astype(jnp.bfloat16), green_matrix) + smooth(
                smooth_res
            )
            fresh_sq = column_squares(gradient)
            direction = gradient + (fresh_sq / grad_sq)[:, None] * direction
            grad_sq = fresh_sq
    return (solution, residual)


MESH = pl.DeviceIdType.MESH


def to_row(column):
    count = column.shape[0]
    eye = lax.broadcasted_iota(jnp.int32, (count, LANES), 0) == lax.broadcasted_iota(
        jnp.int32, (count, LANES), 1
    )
    return jnp.sum(jnp.where(eye, jnp.broadcast_to(column, (count, LANES)), 0.0), axis=0, keepdims=True)


def to_column(row, count):
    eye = lax.broadcasted_iota(jnp.int32, (count, LANES), 0) == lax.broadcasted_iota(
        jnp.int32, (count, LANES), 1
    )
    return jnp.sum(jnp.where(eye, jnp.broadcast_to(row, (count, LANES)), 0.0), axis=1, keepdims=True)


def flipped(index, mask, count):
    value, bit = 0, 1
    while bit < count:
        digit = lax.rem(index // bit, 2)
        value = value + bit * (1 - digit if mask & bit else digit)
        bit *= 2
    return value


def far_first(count):
    masks = []
    bit = count // 2
    while bit:
        masks += range(bit, 2 * bit)
        bit //= 2
    return masks


def stencil(above, here, below):
    lane = lax.broadcasted_iota(jnp.int32, here.shape, 1)
    left = jnp.where(lane == 0, 0.0, pltpu.roll(here, 1, 1))
    right = jnp.where(lane == GRID - 1, 0.0, pltpu.roll(here, GRID - 1, 1))
    return here - 0.25 * (above + below + left + right)


def cgls_kernel(
    nz, npar,
    green_hbm, obs_ref, x_ref, r_ref,
    green, imb, im, p_ext, sp, g_own, own_part, gg_ref,
    rs_send, rs_recv, ag, y_send, y_recv, h_recv, halo,
    sz, sp_scalar, nz_scalar, npar_scalar,
    load_sem, rs_ss, rs_rs, ag_ss, ag_rs, relay_ss, y_ss, y_rs, h_ss, h_rs, halo_ss, halo_rs,
    sz_ss, sz_rs, sp_ss, sp_rs, nz_ss, nz_rs, np_ss, np_rs,
):
    me_z = lax.axis_index("pix")
    me_p = lax.axis_index("par")
    core = lax.rem(me_p, 2)
    chip = me_p // 2
    nchip = npar // 2
    partner = me_p + 1 - 2 * core
    sets = obs_ref.shape[0]
    half = sets // 2
    width = green.shape[3]
    rows = nz * SUB * width // GRID
    own_rows = width // GRID
    edge = 2 * GRID
    z_peers = [flipped(me_z, mask, nz) for mask in far_first(nz)]
    z_from = z_peers[::-1]
    p_peers = [lax.rem(me_p + j, npar) for j in range(1, npar)]
    order = [(s, c) for s in range(SUB) for c in z_peers] + [(s, me_z) for s in range(SUB)]

    def load(s, c):
        first = pl.multiple_of((c * SUB + s) * width, width)
        return pltpu.make_async_copy(
            green_hbm.at[:, pl.ds(first, width)], green.at[c, s], load_sem.at[c, s]
        )

    for s, c in order:
        load(s, c).start()

    barrier = pltpu.get_barrier_semaphore()
    for j in range(1, nz):
        pl.semaphore_signal(barrier, inc=1, device_id={"pix": lax.rem(me_z + j, nz)}, device_id_type=MESH)
    for j in range(1, npar):
        pl.semaphore_signal(barrier, inc=1, device_id={"par": lax.rem(me_p + j, npar)}, device_id_type=MESH)

    imb[...] = obs_ref[...]
    im[...] = jnp.zeros_like(im)
    p_ext[...] = jnp.zeros_like(p_ext)
    g_own[...] = jnp.zeros_like(g_own)
    gg_ref[...] = jnp.zeros_like(gg_ref)
    x_ref[...] = jnp.zeros_like(x_ref)
    r_ref[...] = obs_ref[...].astype(jnp.float32)

    pl.semaphore_wait(barrier, nz + npar - 2)

    def to_z(buf, k, ssem, rsem, peer, s=0):
        return pltpu.make_async_remote_copy(
            src_ref=buf.at[k, me_z, s], dst_ref=buf.at[k, me_z, s],
            send_sem=ssem.at[k, peer, s], recv_sem=rsem.at[k, me_z, s],
            device_id={"pix": peer}, device_id_type=MESH,
        )

    def from_z(buf, k, ssem, rsem, peer, s=0):
        return pltpu.make_async_remote_copy(
            src_ref=buf.at[k, peer, s], dst_ref=buf.at[k, peer, s],
            send_sem=ssem.at[k, peer, s], recv_sem=rsem.at[k, peer, s],
            device_id={"pix": peer}, device_id_type=MESH,
        )

    def to_par(buf, k, ssem, rsem, peer):
        return pltpu.make_async_remote_copy(
            src_ref=buf.at[k, me_p], dst_ref=buf.at[k, me_p],
            send_sem=ssem.at[k, peer], recv_sem=rsem.at[k, me_p],
            device_id={"par": peer}, device_id_type=MESH,
        )

    def from_par(buf, k, ssem, rsem, peer):
        return pltpu.make_async_remote_copy(
            src_ref=buf.at[k, peer], dst_ref=buf.at[k, peer],
            send_sem=ssem.at[k, peer], recv_sem=rsem.at[k, peer],
            device_id={"par": peer}, device_id_type=MESH,
        )


    def total_row(parts):
        value = parts[0]
        for part in parts[1:]:
            value = value + part
        return value

    def z_row(buf, k):
        return total_row([buf[k, i, 0, 0:1] for i in range(nz)])

    def par_row(buf, k):
        return total_row([buf[k, i, 0:1] for i in range(npar)])

    def send_image_sq(k):
        image = im[...]
        row = to_row(jnp.sum(image * image, axis=1, keepdims=True))
        sz[k, me_z, 0] = jnp.broadcast_to(row, (8, LANES))
        for peer in z_peers:
            to_z(sz, k, sz_ss, sz_rs, peer).start()

    def send_smooth_sq(k):
        square = jnp.zeros((sets, GRID), jnp.float32)
        for i in range(rows + 2):
            line = stencil(
                p_ext[:, i * GRID:(i + 1) * GRID],
                p_ext[:, (i + 1) * GRID:(i + 2) * GRID],
                p_ext[:, (i + 2) * GRID:(i + 3) * GRID],
            )
            if i == 0:
                line = jnp.where(me_p == 0, 0.0, line)
            elif i == rows + 1:
                line = jnp.where(me_p == npar - 1, 0.0, line)
            else:
                square = square + line * line
            sp[:, i * GRID:(i + 1) * GRID] = line
        row = to_row(jnp.sum(square, axis=1, keepdims=True))
        sp_scalar[k, me_p] = jnp.broadcast_to(row, (8, LANES))
        for peer in p_peers:
            to_par(sp_scalar, k, sp_ss, sp_rs, peer).start()

    def curvature(k):
        for peer in p_peers:
            from_par(sp_scalar, k, sp_ss, sp_rs, peer).wait_recv()
        for peer in z_from:
            from_z(sz, k, sz_ss, sz_rs, peer).wait_recv()
        return z_row(sz, k) + par_row(sp_scalar, k)

    def apply_step(step):
        x_ref[...] += step * p_ext[:, edge:edge + rows * GRID]
        r_ref[...] -= step * im[...]

    def finish_scalars(k):
        for peer in z_peers:
            to_z(sz, k, sz_ss, sz_rs, peer).wait_send()
        for peer in p_peers:
            to_par(sp_scalar, k, sp_ss, sp_rs, peer).wait_send()

    def rs_copy(k, target, s):
        return pltpu.make_async_remote_copy(
            src_ref=rs_send.at[k, target, s], dst_ref=rs_recv.at[k, me_z, s],
            send_sem=rs_ss.at[k, target, s], recv_sem=rs_rs.at[k, me_z, s],
            device_id={"pix": target}, device_id_type=MESH,
        )

    def rs_from(k, source, s):
        return pltpu.make_async_remote_copy(
            src_ref=rs_send.at[k, source, s], dst_ref=rs_recv.at[k, source, s],
            send_sem=rs_ss.at[k, source, s], recv_sem=rs_rs.at[k, source, s],
            device_id={"pix": source}, device_id_type=MESH,
        )

    def relay_masks(s):
        if s + 1 == SUB:
            return []
        return [mask for mask in far_first(nz) if mask % 2 == 0]

    def sent_masks(s):
        if s + 1 == SUB:
            return far_first(nz)
        return [mask for mask in far_first(nz) if mask % 2 == 0 or mask == 1]

    def relay(k, source, s):
        mate = flipped(me_z, 1, nz)
        return pltpu.make_async_remote_copy(
            src_ref=ag.at[k, source, s], dst_ref=ag.at[k, source, s],
            send_sem=relay_ss.at[k, source, s], recv_sem=ag_rs.at[k, source, s],
            device_id={"pix": mate}, device_id_type=MESH,
        )

    up = lax.rem(me_p + 1, npar)
    down = lax.rem(me_p + npar - 1, npar)

    def halo_copies(k):
        return (
            pltpu.make_async_remote_copy(
                src_ref=ag.at[k, nz - 1, SUB - 1, :, pl.ds(width - edge, edge)], dst_ref=halo.at[k, 0],
                send_sem=halo_ss.at[k, 0], recv_sem=halo_rs.at[k, 0],
                device_id={"par": up}, device_id_type=MESH,
            ),
            pltpu.make_async_remote_copy(
                src_ref=ag.at[k, 0, 0, :, pl.ds(0, edge)], dst_ref=halo.at[k, 1],
                send_sem=halo_ss.at[k, 1], recv_sem=halo_rs.at[k, 1],
                device_id={"par": down}, device_id_type=MESH,
            ),
        )

    def y_copy(k):
        return pltpu.make_async_remote_copy(
            src_ref=y_send.at[k], dst_ref=y_recv.at[k],
            send_sem=y_ss.at[k], recv_sem=y_rs.at[k],
            device_id={"par": partner}, device_id_type=MESH,
        )

    @pl.loop(0, ITERS)
    def _(k):
        send_image_sq(k)
        vector = imb[...]

        def backward(s, c):
            @pl.when(k == 0)
            def _():
                load(s, c).wait()

            return jnp.dot(vector, green[c, s], preferred_element_type=jnp.float32)

        for s in range(SUB):
            for peer in z_peers:
                rs_send[k, peer, s] = backward(s, peer).astype(jnp.bfloat16)
                rs_copy(k, peer, s).start()
        send_smooth_sq(k)
        for s in range(SUB):
            base = (me_z * SUB + s) * own_rows
            lines = []
            for i in range(own_rows):
                lines.append(stencil(*[
                    sp[:, pl.ds(pl.multiple_of((base + i + d) * GRID, GRID), GRID)]
                    for d in range(3)
                ]))
            own_part[s] = backward(s, me_z) + jnp.concatenate(lines, axis=1)
        step = jnp.where(k == 0, -1.0, gg_ref[0:1] / curvature(k))
        step = to_column(step, sets)
        square = jnp.zeros((sets, 1), jnp.float32)
        for s in range(SUB):
            fresh = own_part[s]
            for source in z_from:
                rs_from(k, source, s).wait_recv()
                fresh = fresh + rs_recv[k, source, s].astype(jnp.float32)
            gradient = g_own[s] - step * fresh
            g_own[s] = gradient
            ag[k, me_z, s] = gradient.astype(jnp.bfloat16)
            for mask in sent_masks(s):
                to_z(ag, k, ag_ss, ag_rs, flipped(me_z, mask, nz), s).start()
            square = square + jnp.sum(gradient * gradient, axis=1, keepdims=True)
        nz_scalar[k, me_z, 0] = jnp.broadcast_to(to_row(square), (8, LANES))
        for peer in z_peers:
            to_z(nz_scalar, k, nz_ss, nz_rs, peer).start()
        apply_step(step)

        def forward(s, c):
            return lax.dot_general(
                ag[k, c, s], green[c, s], (((1,), (1,)), ((), ())),
                preferred_element_type=jnp.float32,
            )

        image = jnp.zeros(im.shape, jnp.float32)
        for s in range(SUB):
            image = image + forward(s, me_z)
        for s in range(SUB):
            for mask in relay_masks(s):
                source = flipped(me_z, mask, nz)
                from_z(ag, k, ag_ss, ag_rs, source, s).wait_recv()
                relay(k, source, s).start()
        for s in range(SUB):
            for mask in sent_masks(s)[::-1]:
                source = flipped(me_z, mask, nz)
                if mask not in relay_masks(s):
                    from_z(ag, k, ag_ss, ag_rs, source, s).wait_recv()
                image = image + forward(s, source)
            if s + 2 <= SUB:
                continue
            for t in range(SUB):
                for mask in relay_masks(t):
                    source = flipped(me_z, mask + 1, nz)
                    from_z(ag, k, ag_ss, ag_rs, source, t).wait_recv()
                    image = image + forward(t, source)
        low, high = image[:half], image[half:]
        mine = jnp.where(core == 0, low, high)
        y_send[k] = jnp.where(core == 0, high, low).astype(jnp.bfloat16)
        y_copy(k).start()
        for source in z_from:
            from_z(nz_scalar, k, nz_ss, nz_rs, source).wait_recv()
        npar_scalar[k, me_p] = jnp.broadcast_to(z_row(nz_scalar, k), (8, LANES))
        for peer in p_peers:
            to_par(npar_scalar, k, np_ss, np_rs, peer).start()
        for copy in halo_copies(k):
            copy.start()
        y_copy(k).wait_recv()
        h_recv[k, me_p] = (mine + y_recv[k].astype(jnp.float32)).astype(jnp.bfloat16)
        for peer in p_peers:
            to_par(h_recv, k, h_ss, h_rs, peer).start()

        for peer in p_peers:
            from_par(npar_scalar, k, np_ss, np_rs, peer).wait_recv()
        fresh_sq = par_row(npar_scalar, k)
        ratio = to_column(jnp.where(k == 0, 0.0, fresh_sq / gg_ref[0:1]), sets)
        gg_ref[...] = jnp.broadcast_to(fresh_sq, gg_ref.shape)
        for copy in halo_copies(k):
            copy.wait_recv()
        for c in range(nz):
            for s in range(SUB):
                first = edge + (c * SUB + s) * width
                where = slice(first, first + width)
                p_ext[:, where] = ag[k, c, s].astype(jnp.float32) + ratio * p_ext[:, where]
        first = jnp.where(me_p == 0, 0.0, halo[k, 0].astype(jnp.float32))
        p_ext[:, :edge] = first + ratio * p_ext[:, :edge]
        last = jnp.where(me_p == npar - 1, 0.0, halo[k, 1].astype(jnp.float32))
        p_ext[:, edge + rows * GRID:] = last + ratio * p_ext[:, edge + rows * GRID:]

        for peer in p_peers:
            from_par(h_recv, k, h_ss, h_rs, peer).wait_recv()
        for c in range(2):
            part = h_recv[k, c].astype(jnp.float32)
            for i in range(1, nchip):
                part = part + h_recv[k, 2 * i + c].astype(jnp.float32)
            where = slice(c * half, (c + 1) * half)
            im[where] = part + ratio[where] * im[where]
        imb[...] = im[...].astype(jnp.bfloat16)

        finish_scalars(k)
        for peer in z_peers:
            for s in range(SUB):
                rs_copy(k, peer, s).wait_send()
            to_z(nz_scalar, k, nz_ss, nz_rs, peer).wait_send()
        for s in range(SUB):
            for mask in sent_masks(s):
                to_z(ag, k, ag_ss, ag_rs, flipped(me_z, mask, nz), s).wait_send()
            for mask in relay_masks(s):
                relay(k, flipped(me_z, mask, nz), s).wait_send()
        y_copy(k).wait_send()
        for copy in halo_copies(k):
            copy.wait_send()
        for peer in p_peers:
            to_par(npar_scalar, k, np_ss, np_rs, peer).wait_send()
            to_par(h_recv, k, h_ss, h_rs, peer).wait_send()

    send_image_sq(ITERS)
    send_smooth_sq(ITERS)
    step = to_column(gg_ref[0:1] / curvature(ITERS), sets)
    apply_step(step)
    finish_scalars(ITERS)


def finish_kernel(x_ref, r_ref, x_out, r_out, x_sem, r_sem):
    copies = (
        pltpu.make_async_copy(x_ref, x_out, x_sem),
        pltpu.make_async_copy(r_ref, r_out, r_sem),
    )
    for copy in copies:
        copy.start()
    for copy in copies:
        copy.wait()


def finish(x, r):
    vmem = pl.BlockSpec(memory_space=pltpu.VMEM)
    space = pl.BlockSpec(memory_space=pl.ANY)
    return pl.pallas_call(
        finish_kernel,
        out_shape=(jax.ShapeDtypeStruct(x.shape, x.dtype), jax.ShapeDtypeStruct(r.shape, r.dtype)),
        in_specs=[vmem, vmem],
        out_specs=(space, space),
        scratch_shapes=[pltpu.SemaphoreType.DMA, pltpu.SemaphoreType.DMA],
    )(x, r)


def on_device_kernel(nz, npar, green_matrix, observed):
    sets, pixels = observed.shape
    cells = green_matrix.shape[1]
    width = cells // (nz * SUB)
    half = sets // 2
    bf16, f32 = jnp.bfloat16, jnp.float32
    dma = pltpu.SemaphoreType.DMA
    n = ITERS
    vmem = pl.BlockSpec(memory_space=pltpu.VMEM)
    return pl.pallas_call(
        functools.partial(cgls_kernel, nz, npar),
        out_shape=(
            jax.ShapeDtypeStruct((sets, cells), f32),
            jax.ShapeDtypeStruct((sets, pixels), f32),
        ),
        in_specs=[pl.BlockSpec(memory_space=pl.ANY), vmem],
        out_specs=(vmem, vmem),
        scratch_shapes=[
            pltpu.VMEM((nz, SUB, pixels, width), bf16),
            pltpu.VMEM((sets, pixels), bf16),
            pltpu.VMEM((sets, pixels), f32),
            pltpu.VMEM((sets, cells + 4 * GRID), f32),
            pltpu.VMEM((sets, cells + 2 * GRID), f32),
            pltpu.VMEM((SUB, sets, width), f32),
            pltpu.VMEM((SUB, sets, width), f32),
            pltpu.VMEM((8, LANES), f32),
            pltpu.VMEM((n, nz, SUB, sets, width), bf16),
            pltpu.VMEM((n, nz, SUB, sets, width), bf16),
            pltpu.VMEM((n, nz, SUB, sets, width), bf16),
            pltpu.VMEM((n, half, pixels), bf16),
            pltpu.VMEM((n, half, pixels), bf16),
            pltpu.VMEM((n, npar, half, pixels), bf16),
            pltpu.VMEM((n, 2, sets, 2 * GRID), bf16),
            pltpu.VMEM((n + 1, nz, 1, 8, LANES), f32),
            pltpu.VMEM((n + 1, npar, 8, LANES), f32),
            pltpu.VMEM((n, nz, 1, 8, LANES), f32),
            pltpu.VMEM((n, npar, 8, LANES), f32),
            dma((nz, SUB)),
            dma((n, nz, SUB)), dma((n, nz, SUB)),
            dma((n, nz, SUB)), dma((n, nz, SUB)),
            dma((n, nz, SUB)),
            dma((n,)), dma((n,)),
            dma((n, npar)), dma((n, npar)),
            dma((n, 2)), dma((n, 2)),
            dma((n + 1, nz, 1)), dma((n + 1, nz, 1)),
            dma((n + 1, npar)), dma((n + 1, npar)),
            dma((n, nz, 1)), dma((n, nz, 1)),
            dma((n, npar)), dma((n, npar)),
        ],
        compiler_params=pltpu.CompilerParams(
            collective_id=0, has_side_effects=True, vmem_limit_bytes=60 * 1024 * 1024
        ),
    )(green_matrix, observed)


def solution(mesh):
    nz, npar = mesh.shape["pix"], mesh.shape["par"]

    def step(green_matrix, observed):
        sets, cells = observed.shape[0], green_matrix.shape[1]
        width = cells // (nz * SUB)
        fits = cells % (nz * SUB * GRID) == 0 and width >= 2 * GRID and nz & (nz - 1) == 0
        if fits and nz > 1 and npar % 2 == 0 and sets % 32 == 0 and sets <= LANES:
            return finish(*on_device_kernel(nz, npar, green_matrix, observed))
        return on_device(green_matrix, observed)

    return jax.shard_map(
        step,
        mesh=mesh,
        in_specs=(P("pix", "par"), P("parts", "pix")),
        out_specs=(P("parts", "par"), P("parts", "pix")),
        check_vma=False,
    )
```

profile of v0, /device:TPU:0, one launch (start us, length us, event | category | flops | bytes accessed | tf_op | source)
XLA Modules:
  0.0 111.8 jit_solution(8964606571877475574)
XLA Ops:
  0.6 109.2 %shard_map.41 = (f32[32,4096]{1,0:T(8,128)}, f32[32,1152]{1,0:T(8,128)}) custom-call(bf16[1152,4096]{1,0:T(8,128)(2,1)} %green_hbm.1, bf16[32,1152]{1,0:T(8,128)(2,1)} %obs_ref.1), custom_call_target="tpu_custom_call" | custom-call | tf_op jit(solution)/shard_map/pallas_call | solution.py:497
  109.9 1.9 %shard_map.42 = (f32[32,4096]{1,0:T(8,128)}, f32[32,1152]{1,0:T(8,128)}) custom-call(f32[32,4096]{1,0:T(8,128)} %get-tuple-element.4.x_ref, f32[32,1152]{1,0:T(8,128)} %get-tuple-element.5.r_ref), custom_call_target="tpu_custom_call" | custom-call | tf_op jit(solution)/shard_map/pallas_call | solution.py:479
where the time goes:
time: 112 us
  Pallas kernels  111 us (99%)
    pallas_call x1, Pallas kernels, on_device_kernel(): pl.pallas_call(functools.partial(cgls_kernel, nz, npar), out_shape=(jax.S...  109 us

commit v1 on v0

v1 whole, which is shorter than its diff:
```python
import functools

import jax
import jax.numpy as jnp
from jax import lax
from jax.experimental import pallas as pl
from jax.experimental.pallas import tpu as pltpu
from jax.sharding import PartitionSpec as P

GRID = 128
ITERS = 5
LANES = 128
SUB = 2
GROUPS = 2
RELAYS = {}


def padded_2(block, sides, width):
    for axis, dim in sides:
        count = lax.axis_size(axis)
        forward = [(i, i + 1) for i in range(count - 1)]
        backward = [(target, source) for source, target in forward]
        low = lax.ppermute(
            lax.slice_in_dim(block, block.shape[dim] - width, None, axis=dim), axis, forward
        )
        high = lax.ppermute(lax.slice_in_dim(block, 0, width, axis=dim), axis, backward)
        block = jnp.concatenate([low, block, high], axis=dim)
    return block


def smooth(values):
    set_count = values.shape[0]
    grid_rows = values.shape[1] // GRID
    tiles = values.reshape(set_count, grid_rows, GRID)
    padded = padded_2(tiles, (("par", 1),), 1)
    padded = jnp.pad(padded, ((0, 0), (0, 0), (1, 1)))
    beside_all = (
        padded[:, 2:, 1:-1] + padded[:, :-2, 1:-1] + padded[:, 1:-1, 2:] + padded[:, 1:-1, :-2]
    )
    return (0.25 * (4.0 * tiles - beside_all)).reshape(set_count, grid_rows * GRID)


def forward(rounded, green_matrix):
    partial_value = lax.dot_general(
        rounded, green_matrix, (((1,), (1,)), ((), ())), preferred_element_type=jnp.float32
    )
    return lax.psum(partial_value, "par")


def curvatures(image, smoothed):
    local_image = jnp.sum(image * image, axis=1)
    local_smooth = jnp.sum(smoothed * smoothed, axis=1)
    image_sq = lax.psum(local_image, "pix")
    smooth_sq = lax.psum(local_smooth, "par")
    return image_sq + smooth_sq


def backward_sum(rounded, green_matrix):
    return lax.psum(jnp.dot(rounded, green_matrix, preferred_element_type=jnp.float32), "pix")


def column_squares(gradient):
    return lax.psum(jnp.sum(gradient * gradient, axis=1), "par")


def on_device(green_matrix, observed):
    set_count = observed.shape[0]
    tile_cells = green_matrix.shape[1]
    residual = observed.astype(jnp.float32)
    gradient = backward_sum(observed, green_matrix)
    grad_sq = column_squares(gradient)
    direction = gradient
    solution = jnp.zeros((set_count, tile_cells), jnp.float32)
    smooth_res = jnp.zeros((set_count, tile_cells), jnp.float32)
    for sweep in range(ITERS):
        rounded = direction.astype(jnp.bfloat16)
        image = forward(rounded, green_matrix)
        smoothed = smooth(lax.optimization_barrier(rounded).astype(jnp.float32))
        step_len = (grad_sq / curvatures(image, smoothed))[:, None]
        solution = solution + step_len * direction
        residual = residual - step_len * image
        smooth_res = smooth_res - step_len * smoothed
        if sweep + 1 < ITERS:
            gradient = backward_sum(residual.astype(jnp.bfloat16), green_matrix) + smooth(
                smooth_res
            )
            fresh_sq = column_squares(gradient)
            direction = gradient + (fresh_sq / grad_sq)[:, None] * direction
            grad_sq = fresh_sq
    return (solution, residual)


MESH = pl.DeviceIdType.MESH


def to_row(column):
    count = column.shape[0]
    eye = lax.broadcasted_iota(jnp.int32, (count, LANES), 0) == lax.broadcasted_iota(
        jnp.int32, (count, LANES), 1
    )
    return jnp.sum(jnp.where(eye, jnp.broadcast_to(column, (count, LANES)), 0.0), axis=0, keepdims=True)


def to_column(row, count):
    eye = lax.broadcasted_iota(jnp.int32, (count, LANES), 0) == lax.broadcasted_iota(
        jnp.int32, (count, LANES), 1
    )
    return jnp.sum(jnp.where(eye, jnp.broadcast_to(row, (count, LANES)), 0.0), axis=1, keepdims=True)


def flipped(index, mask, count):
    value, bit = 0, 1
    while bit < count:
        digit = lax.rem(index // bit, 2)
        value = value + bit * (1 - digit if mask & bit else digit)
        bit *= 2
    return value


def far_first(count):
    masks = []
    bit = count // 2
    while bit:
        masks += range(bit, 2 * bit)
        bit //= 2
    return masks


def stencil(above, here, below):
    lane = lax.broadcasted_iota(jnp.int32, here.shape, 1)
    left = jnp.where(lane == 0, 0.0, pltpu.roll(here, 1, 1))
    right = jnp.where(lane == GRID - 1, 0.0, pltpu.roll(here, GRID - 1, 1))
    return here - 0.25 * (above + below + left + right)


def cgls_kernel(
    nz, npar,
    green_hbm, obs_ref, x_ref, r_ref,
    green, imb, im, own_image, p_ext, sp, g_own, own_part, gg_ref,
    rs_send, rs_recv, ag, h_recv, halo,
    sz, sp_scalar, nz_scalar, npar_scalar,
    load_sem, rs_ss, rs_rs, ag_ss, ag_rs, relay_ss, h_ss, h_rs, halo_ss, halo_rs,
    sz_ss, sz_rs, sp_ss, sp_rs, nz_ss, nz_rs, np_ss, np_rs,
):
    me_z = lax.axis_index("pix")
    me_p = lax.axis_index("par")
    core = lax.rem(me_p, 2)
    chip = me_p // 2
    nchip = npar // 2
    partner = me_p + 1 - 2 * core
    size = obs_ref.shape[0] // GROUPS
    groups = range(GROUPS)
    width = green.shape[3]
    rows = nz * SUB * width // GRID
    own_rows = width // GRID
    edge = 2 * GRID
    z_peers = [flipped(me_z, mask, nz) for mask in far_first(nz)]
    z_from = z_peers[::-1]
    p_peers = [
        2 * lax.rem(chip + i, nchip) + c for i in range(1, nchip) for c in range(2)
    ] + [partner]
    order = [(s, c) for s in range(SUB) for c in z_peers] + [(s, me_z) for s in range(SUB)]

    def load(s, c):
        first = pl.multiple_of((c * SUB + s) * width, width)
        return pltpu.make_async_copy(
            green_hbm.at[:, pl.ds(first, width)], green.at[c, s], load_sem.at[c, s]
        )

    for s, c in order:
        load(s, c).start()

    barrier = pltpu.get_barrier_semaphore()
    for j in range(1, nz):
        pl.semaphore_signal(barrier, inc=1, device_id={"pix": lax.rem(me_z + j, nz)}, device_id_type=MESH)
    for j in range(1, npar):
        pl.semaphore_signal(barrier, inc=1, device_id={"par": lax.rem(me_p + j, npar)}, device_id_type=MESH)

    for g in groups:
        mine = slice(g * size, (g + 1) * size)
        imb[g] = obs_ref[mine]
        r_ref[mine] = obs_ref[mine].astype(jnp.float32)
    im[...] = jnp.zeros_like(im)
    p_ext[...] = jnp.zeros_like(p_ext)
    sp[...] = jnp.zeros_like(sp)
    sz[0] = jnp.zeros_like(sz[0])
    sp_scalar[0] = jnp.zeros_like(sp_scalar[0])
    g_own[...] = jnp.zeros_like(g_own)
    gg_ref[...] = jnp.zeros_like(gg_ref)
    x_ref[...] = jnp.zeros_like(x_ref)

    with jax.named_scope("barrier"):
        pl.semaphore_wait(barrier, nz + npar - 2)

    def z_copy(buf, ssem, rsem, k, g, source, target, *s):
        return pltpu.make_async_remote_copy(
            src_ref=buf.at[(k, g, source, *s)], dst_ref=buf.at[(k, g, source, *s)],
            send_sem=ssem.at[(k, g, target, *s)], recv_sem=rsem.at[(k, g, source, *s)],
            device_id={"pix": target}, device_id_type=MESH,
        )

    def to_z(buf, ssem, rsem, k, g, peer, *s):
        return z_copy(buf, ssem, rsem, k, g, me_z, peer, *s)

    def from_z(buf, ssem, rsem, k, g, peer, *s):
        return z_copy(buf, ssem, rsem, k, g, peer, peer, *s)

    def par_copy(buf, ssem, rsem, k, g, source, target):
        return pltpu.make_async_remote_copy(
            src_ref=buf.at[k, g, source], dst_ref=buf.at[k, g, source],
            send_sem=ssem.at[k, g, target], recv_sem=rsem.at[k, g, source],
            device_id={"par": target}, device_id_type=MESH,
        )

    def to_par(buf, ssem, rsem, k, g, peer):
        return par_copy(buf, ssem, rsem, k, g, me_p, peer)

    def from_par(buf, ssem, rsem, k, g, peer):
        return par_copy(buf, ssem, rsem, k, g, peer, peer)

    image_sq = (sz, sz_ss, sz_rs)
    smooth_sq = (sp_scalar, sp_ss, sp_rs)
    pix_sq = (nz_scalar, nz_ss, nz_rs)
    par_sq = (npar_scalar, np_ss, np_rs)
    gathered = (ag, ag_ss, ag_rs)
    images = (h_recv, h_ss, h_rs)

    def total_row(parts):
        value = parts[0]
        for part in parts[1:]:
            value = value + part
        return value

    def z_row(buf, k, g):
        return total_row([buf[k, g, i, 0:1] for i in range(nz)])

    def par_row(buf, k, g):
        return total_row([buf[k, g, i, 0:1] for i in range(npar)])

    def send_image_sq(k, g):
        image = im[g]
        row = to_row(jnp.sum(image * image, axis=1, keepdims=True))
        sz[k, g, me_z] = jnp.broadcast_to(row, (8, LANES))
        for peer in z_peers:
            to_z(*image_sq, k, g, peer).start()

    def send_smooth_sq(k, g):
        square = jnp.zeros((size, GRID), jnp.float32)
        for i in range(rows + 2):
            line = stencil(
                p_ext[g, :, i * GRID:(i + 1) * GRID],
                p_ext[g, :, (i + 1) * GRID:(i + 2) * GRID],
                p_ext[g, :, (i + 2) * GRID:(i + 3) * GRID],
            )
            if i == 0:
                line = jnp.where(me_p == 0, 0.0, line)
            elif i == rows + 1:
                line = jnp.where(me_p == npar - 1, 0.0, line)
            else:
                square = square + line * line
            sp[g, :, i * GRID:(i + 1) * GRID] = line
        row = to_row(jnp.sum(square, axis=1, keepdims=True))
        sp_scalar[k, g, me_p] = jnp.broadcast_to(row, (8, LANES))
        for peer in p_peers:
            to_par(*smooth_sq, k, g, peer).start()

    def wait_curvature(k, g):
        for peer in p_peers:
            from_par(*smooth_sq, k, g, peer).wait_recv()
        for peer in z_from:
            from_z(*image_sq, k, g, peer).wait_recv()

    def step_row(k, g):
        return gg_ref[g, 0:1] / (z_row(sz, k, g) + par_row(sp_scalar, k, g))

    def apply_step(step, g):
        mine = slice(g * size, (g + 1) * size)
        x_ref[mine] += step * p_ext[g, :, edge:edge + rows * GRID]
        r_ref[mine] -= step * im[g]

    def finish_curvature(k, g):
        for peer in z_peers:
            to_z(*image_sq, k, g, peer).wait_send()
        for peer in p_peers:
            to_par(*smooth_sq, k, g, peer).wait_send()

    def rs_copy(k, g, target, s):
        return pltpu.make_async_remote_copy(
            src_ref=rs_send.at[k, g, target, s], dst_ref=rs_recv.at[k, g, me_z, s],
            send_sem=rs_ss.at[k, g, target, s], recv_sem=rs_rs.at[k, g, me_z, s],
            device_id={"pix": target}, device_id_type=MESH,
        )

    def rs_from(k, g, source, s):
        return pltpu.make_async_remote_copy(
            src_ref=rs_send.at[k, g, source, s], dst_ref=rs_recv.at[k, g, source, s],
            send_sem=rs_ss.at[k, g, source, s], recv_sem=rs_rs.at[k, g, source, s],
            device_id={"pix": source}, device_id_type=MESH,
        )

    def relayed(g, s):
        return (g, s) in RELAYS

    def sent_to(g, s):
        return [flipped(me_z, mask, nz) for mask in far_first(nz) if not relayed(g, s) or mask != 3]

    def relay_copy(k, g, s):
        cross = flipped(me_z, 2, nz)
        return z_copy(ag, relay_ss, ag_rs, k, g, cross, flipped(me_z, 1, nz), s)

    def relays(k, point):
        for (g, s), place in RELAYS.items():
            if place == point:
                with jax.named_scope("relay%d" % g):
                    from_z(*gathered, k, g, flipped(me_z, 2, nz), s).wait_recv()
                    relay_copy(k, g, s).start()

    up = lax.rem(me_p + 1, npar)
    down = lax.rem(me_p + npar - 1, npar)

    def halo_copies(k, g):
        return (
            pltpu.make_async_remote_copy(
                src_ref=ag.at[k, g, nz - 1, SUB - 1, :, pl.ds(width - edge, edge)],
                dst_ref=halo.at[k, g, 0],
                send_sem=halo_ss.at[k, g, 0], recv_sem=halo_rs.at[k, g, 0],
                device_id={"par": up}, device_id_type=MESH,
            ),
            pltpu.make_async_remote_copy(
                src_ref=ag.at[k, g, 0, 0, :, pl.ds(0, edge)],
                dst_ref=halo.at[k, g, 1],
                send_sem=halo_ss.at[k, g, 1], recv_sem=halo_rs.at[k, g, 1],
                device_id={"par": down}, device_id_type=MESH,
            ),
        )

    def scatter(k, g):
        vector = imb[g]

        def backward(s, c):
            if g == 0:
                @pl.when(k == 0)
                def _():
                    load(s, c).wait()

            return jnp.dot(vector, green[c, s], preferred_element_type=jnp.float32)

        with jax.named_scope("bwd%d" % g):
            for s in range(SUB):
                for peer in z_peers:
                    rs_send[k, g, peer, s] = backward(s, peer).astype(jnp.bfloat16)
                    rs_copy(k, g, peer, s).start()
        with jax.named_scope("own%d" % g):
            for s in range(SUB):
                base = (me_z * SUB + s) * own_rows
                lines = []
                for i in range(own_rows):
                    lines.append(stencil(*[
                        sp[g, :, pl.ds(pl.multiple_of((base + i + d) * GRID, GRID), GRID)]
                        for d in range(3)
                    ]))
                own_part[g, s] = backward(s, me_z) + jnp.concatenate(lines, axis=1)

    def gather(k, g):
        with jax.named_scope("curv%d" % g):
            @pl.when(k > 0)
            def _():
                wait_curvature(k, g)

            step = to_column(jnp.where(k == 0, -1.0, step_row(k, g)), size)
        square = jnp.zeros((size, 1), jnp.float32)
        for s in range(SUB):
            with jax.named_scope("rs%d" % g):
                for source in z_from:
                    rs_from(k, g, source, s).wait_recv()
            with jax.named_scope("upd%d" % g):
                fresh = own_part[g, s]
                for source in z_from:
                    fresh = fresh + rs_recv[k, g, source, s].astype(jnp.float32)
                gradient = g_own[g, s] - step * fresh
                g_own[g, s] = gradient
                ag[k, g, me_z, s] = gradient.astype(jnp.bfloat16)
                for peer in sent_to(g, s):
                    to_z(*gathered, k, g, peer, s).start()
                square = square + jnp.sum(gradient * gradient, axis=1, keepdims=True)
            relays(k, "g%d%d" % (g, s))
        with jax.named_scope("app%d" % g):
            nz_scalar[k, g, me_z] = jnp.broadcast_to(to_row(square), (8, LANES))
            for peer in z_peers:
                to_z(*pix_sq, k, g, peer).start()
            apply_step(step, g)

    def forward(k, g, s, c):
        return lax.dot_general(
            ag[k, g, c, s], green[c, s], (((1,), (1,)), ((), ())),
            preferred_element_type=jnp.float32,
        )

    def forward_own(k, g):
        with jax.named_scope("fown%d" % g):
            image = forward(k, g, 0, me_z)
            for s in range(1, SUB):
                image = image + forward(k, g, s, me_z)
            own_image[g] = image

    def forward_rest(k, g):
        image = own_image[g]
        with jax.named_scope("frest%d" % g):
            seq = [(s, mask) for s in range(SUB) for mask in ((1, 2) if relayed(g, s) else (1, 3, 2))]
            late = [(s, 3) for s in range(SUB) if relayed(g, s)]
            cut = len(seq) - 3
            seq = seq[:cut] + late[:1] + seq[cut:] + late[1:]
            for i, (s, mask) in enumerate(seq):
                source = flipped(me_z, mask, nz)
                if not (relayed(g, s) and mask == 2):
                    from_z(*gathered, k, g, source, s).wait_recv()
                if i + 1 == len(seq):
                    for copy in halo_copies(k, g):
                        copy.start()
                image = image + forward(k, g, s, source)
                relays(k, "f%d%d" % (g, i))
                if i == 2:
                    for source in z_from:
                        from_z(*pix_sq, k, g, source).wait_recv()
                    npar_scalar[k, g, me_p] = jnp.broadcast_to(z_row(nz_scalar, k, g), (8, LANES))
                    for peer in p_peers:
                        to_par(*par_sq, k, g, peer).start()
        with jax.named_scope("hsend%d" % g):
            h_recv[k, g, me_p] = image.astype(jnp.bfloat16)
            for peer in p_peers:
                to_par(*images, k, g, peer).start()

    def advance(k, g):
        with jax.named_scope("npw%d" % g):
            for peer in p_peers:
                from_par(*par_sq, k, g, peer).wait_recv()
            for copy in halo_copies(k, g):
                copy.wait_recv()
        with jax.named_scope("pupd%d" % g):
            fresh_sq = par_row(npar_scalar, k, g)
            ratio = to_column(jnp.where(k == 0, 0.0, fresh_sq / gg_ref[g, 0:1]), size)
            gg_ref[g] = jnp.broadcast_to(fresh_sq, (8, LANES))
            for c in range(nz):
                for s in range(SUB):
                    first = edge + (c * SUB + s) * width
                    where = slice(first, first + width)
                    p_ext[g, :, where] = (
                        ag[k, g, c, s].astype(jnp.float32) + ratio * p_ext[g, :, where]
                    )
            first = jnp.where(me_p == 0, 0.0, halo[k, g, 0].astype(jnp.float32))
            p_ext[g, :, :edge] = first + ratio * p_ext[g, :, :edge]
            last = jnp.where(me_p == npar - 1, 0.0, halo[k, g, 1].astype(jnp.float32))
            p_ext[g, :, edge + rows * GRID:] = last + ratio * p_ext[g, :, edge + rows * GRID:]
            send_smooth_sq(k + 1, g)
        with jax.named_scope("hw%d" % g):
            for peer in p_peers:
                from_par(*images, k, g, peer).wait_recv()
        with jax.named_scope("im%d" % g):
            part = h_recv[k, g, 0].astype(jnp.float32)
            for i in range(1, npar):
                part = part + h_recv[k, g, i].astype(jnp.float32)
            image = part + ratio * im[g]
            im[g] = image
            imb[g] = image.astype(jnp.bfloat16)
            send_image_sq(k + 1, g)

    def finish_sends(k, g):
        for peer in z_peers:
            for s in range(SUB):
                rs_copy(k, g, peer, s).wait_send()
            to_z(*pix_sq, k, g, peer).wait_send()
        for s in range(SUB):
            for peer in sent_to(g, s):
                to_z(*gathered, k, g, peer, s).wait_send()
            if relayed(g, s):
                relay_copy(k, g, s).wait_send()
        for copy in halo_copies(k, g):
            copy.wait_send()
        for peer in p_peers:
            to_par(*par_sq, k, g, peer).wait_send()
            to_par(*images, k, g, peer).wait_send()
        finish_curvature(k + 1, g)

    @pl.loop(0, ITERS)
    def _(k):
        @pl.when(k > 0)
        def _():
            advance(k - 1, 0)

        scatter(k, 0)

        @pl.when(k > 0)
        def _():
            forward_rest(k - 1, 1)
            finish_sends(k - 1, 0)

        gather(k, 0)
        forward_own(k, 0)

        @pl.when(k > 0)
        def _():
            advance(k - 1, 1)

        scatter(k, 1)

        @pl.when(k > 0)
        def _():
            finish_sends(k - 1, 1)

        forward_rest(k, 0)
        gather(k, 1)
        forward_own(k, 1)

    advance(ITERS - 1, 0)
    forward_rest(ITERS - 1, 1)
    with jax.named_scope("final"):
        finish_sends(ITERS - 1, 0)
        wait_curvature(ITERS, 0)
        apply_step(to_column(step_row(ITERS, 0), size), 0)
    advance(ITERS - 1, 1)
    with jax.named_scope("final2"):
        finish_sends(ITERS - 1, 1)
        wait_curvature(ITERS, 1)
        apply_step(to_column(step_row(ITERS, 1), size), 1)


def finish_kernel(x_ref, r_ref, x_out, r_out, x_sem, r_sem):
    copies = (
        pltpu.make_async_copy(x_ref, x_out, x_sem),
        pltpu.make_async_copy(r_ref, r_out, r_sem),
    )
    for copy in copies:
        copy.start()
    for copy in copies:
        copy.wait()


def finish(x, r):
    vmem = pl.BlockSpec(memory_space=pltpu.VMEM)
    space = pl.BlockSpec(memory_space=pl.ANY)
    return pl.pallas_call(
        finish_kernel,
        out_shape=(jax.ShapeDtypeStruct(x.shape, x.dtype), jax.ShapeDtypeStruct(r.shape, r.dtype)),
        in_specs=[vmem, vmem],
        out_specs=(space, space),
        scratch_shapes=[pltpu.SemaphoreType.DMA, pltpu.SemaphoreType.DMA],
    )(x, r)


def on_device_kernel(nz, npar, green_matrix, observed):
    sets, pixels = observed.shape
    cells = green_matrix.shape[1]
    width = cells // (nz * SUB)
    size = sets // GROUPS
    bf16, f32 = jnp.bfloat16, jnp.float32
    dma = pltpu.SemaphoreType.DMA
    n = ITERS
    vmem = pl.BlockSpec(memory_space=pltpu.VMEM)
    return pl.pallas_call(
        functools.partial(cgls_kernel, nz, npar),
        out_shape=(
            jax.ShapeDtypeStruct((sets, cells), f32),
            jax.ShapeDtypeStruct((sets, pixels), f32),
        ),
        in_specs=[pl.BlockSpec(memory_space=pl.ANY), vmem],
        out_specs=(vmem, vmem),
        scratch_shapes=[
            pltpu.VMEM((nz, SUB, pixels, width), bf16),
            pltpu.VMEM((GROUPS, size, pixels), bf16),
            pltpu.VMEM((GROUPS, size, pixels), f32),
            pltpu.VMEM((GROUPS, size, pixels), f32),
            pltpu.VMEM((GROUPS, size, cells + 4 * GRID), f32),
            pltpu.VMEM((GROUPS, size, cells + 2 * GRID), f32),
            pltpu.VMEM((GROUPS, SUB, size, width), f32),
            pltpu.VMEM((GROUPS, SUB, size, width), f32),
            pltpu.VMEM((GROUPS, 8, LANES), f32),
            pltpu.VMEM((n, GROUPS, nz, SUB, size, width), bf16),
            pltpu.VMEM((n, GROUPS, nz, SUB, size, width), bf16),
            pltpu.VMEM((n, GROUPS, nz, SUB, size, width), bf16),
            pltpu.VMEM((n, GROUPS, npar, size, pixels), bf16),
            pltpu.VMEM((n, GROUPS, 2, size, 2 * GRID), bf16),
            pltpu.VMEM((n + 1, GROUPS, nz, 8, LANES), f32),
            pltpu.VMEM((n + 1, GROUPS, npar, 8, LANES), f32),
            pltpu.VMEM((n, GROUPS, nz, 8, LANES), f32),
            pltpu.VMEM((n, GROUPS, npar, 8, LANES), f32),
            dma((nz, SUB)),
            dma((n, GROUPS, nz, SUB)), dma((n, GROUPS, nz, SUB)),
            dma((n, GROUPS, nz, SUB)), dma((n, GROUPS, nz, SUB)),
            dma((n, GROUPS, nz, SUB)),
            dma((n, GROUPS, npar)), dma((n, GROUPS, npar)),
            dma((n, GROUPS, 2)), dma((n, GROUPS, 2)),
            dma((n + 1, GROUPS, nz)), dma((n + 1, GROUPS, nz)),
            dma((n + 1, GROUPS, npar)), dma((n + 1, GROUPS, npar)),
            dma((n, GROUPS, nz)), dma((n, GROUPS, nz)),
            dma((n, GROUPS, npar)), dma((n, GROUPS, npar)),
        ],
        compiler_params=pltpu.CompilerParams(
            collective_id=0, has_side_effects=True, vmem_limit_bytes=60 * 1024 * 1024
        ),
    )(green_matrix, observed)


def solution(mesh):
    nz, npar = mesh.shape["pix"], mesh.shape["par"]

    def step(green_matrix, observed):
        sets, cells = observed.shape[0], green_matrix.shape[1]
        width = cells // (nz * SUB)
        fits = cells % (nz * SUB * GRID) == 0 and width >= 2 * GRID and nz & (nz - 1) == 0
        if fits and nz > 1 and npar % 2 == 0 and sets % 32 == 0 and sets <= LANES:
            return finish(*on_device_kernel(nz, npar, green_matrix, observed))
        return on_device(green_matrix, observed)

    return jax.shard_map(
        step,
        mesh=mesh,
        in_specs=(P("pix", "par"), P("parts", "pix")),
        out_specs=(P("parts", "par"), P("parts", "pix")),
        check_vma=False,
    )
```

time: 112 us -> 106 us (0.946)
  Pallas kernels: 111 us -> 105 us
    pallas_call x1, Pallas kernels: 109 us -> 103 us  [on_device_kernel(): pl.pallas_call(functools.partial(cgls_kernel, nz, npar), out_shape=(jax.S...]
where the time goes in v1:
time: 106 us
  Pallas kernels  105 us (99%)
    pallas_call x1, Pallas kernels, on_device_kernel(): pl.pallas_call(functools.partial(cgls_kernel, nz, npar), out_shape=(jax.S...  103 us

profile of v1, /device:TPU:0, one launch (start us, length us, event | category | flops | bytes accessed | tf_op | source)
XLA Modules:
  0.0 105.9 jit_solution(1881941085885902048)
XLA Ops:
  0.6 103.4 %shard_map.41 = (f32[32,4096]{1,0:T(8,128)}, f32[32,1152]{1,0:T(8,128)}) custom-call(bf16[1152,4096]{1,0:T(8,128)(2,1)} %green_hbm.1, bf16[32,1152]{1,0:T(8,128)(2,1)} %obs_ref.1), custom_call_target="tpu_custom_call" | custom-call | tf_op jit(solution)/shard_map/pallas_call | solution.py:559
  104.0 1.9 %shard_map.42 = (f32[32,4096]{1,0:T(8,128)}, f32[32,1152]{1,0:T(8,128)}) custom-call(f32[32,4096]{1,0:T(8,128)} %get-tuple-element.4.x_ref, f32[32,1152]{1,0:T(8,128)} %get-tuple-element.5.r_ref), custom_call_target="tpu_custom_call" | custom-call | tf_op jit(solution)/shard_map/pallas_call | solution.py:541

commit v2 on v1

--- a/solution.py
+++ b/solution.py
@@ -12,7 +12,6 @@
 LANES = 128
 SUB = 2
 GROUPS = 2
-RELAYS = {}
 
 
 def padded_2(block, sides, width):
@@ -121,7 +120,7 @@
     masks = []
     bit = count // 2
     while bit:
-        masks += range(bit, 2 * bit)
+        masks += range(2 * bit - 1, bit - 1, -1)
         bit //= 2
     return masks
 
@@ -136,10 +135,10 @@
 def cgls_kernel(
     nz, npar,
     green_hbm, obs_ref, x_ref, r_ref,
-    green, imb, im, own_image, p_ext, sp, g_own, own_part, gg_ref,
+    green, green_t, imb, im, own_image, p_ext, sp, g_own, own_part, gg_ref,
     rs_send, rs_recv, ag, h_recv, halo,
     sz, sp_scalar, nz_scalar, npar_scalar,
-    load_sem, rs_ss, rs_rs, ag_ss, ag_rs, relay_ss, h_ss, h_rs, halo_ss, halo_rs,
+    load_sem, rs_ss, rs_rs, ag_ss, ag_rs, h_ss, h_rs, halo_ss, halo_rs,
     sz_ss, sz_rs, sp_ss, sp_rs, nz_ss, nz_rs, np_ss, np_rs,
 ):
     me_z = lax.axis_index("pix")
@@ -298,23 +297,6 @@
             device_id={"pix": source}, device_id_type=MESH,
         )
 
-    def relayed(g, s):
-        return (g, s) in RELAYS
-
-    def sent_to(g, s):
-        return [flipped(me_z, mask, nz) for mask in far_first(nz) if not relayed(g, s) or mask != 3]
-
-    def relay_copy(k, g, s):
-        cross = flipped(me_z, 2, nz)
-        return z_copy(ag, relay_ss, ag_rs, k, g, cross, flipped(me_z, 1, nz), s)
-
-    def relays(k, point):
-        for (g, s), place in RELAYS.items():
-            if place == point:
-                with jax.named_scope("relay%d" % g):
-                    from_z(*gathered, k, g, flipped(me_z, 2, nz), s).wait_recv()
-                    relay_copy(k, g, s).start()
-
     up = lax.rem(me_p + 1, npar)
     down = lax.rem(me_p + npar - 1, npar)
 
@@ -334,15 +316,12 @@
             ),
         )
 
-    def scatter(k, g):
+    def scatter(k, g, loading=False):
         vector = imb[g]
 
         def backward(s, c):
-            if g == 0:
-                @pl.when(k == 0)
-                def _():
-                    load(s, c).wait()
-
+            if loading:
+                load(s, c).wait()
             return jnp.dot(vector, green[c, s], preferred_element_type=jnp.float32)
 
         with jax.named_scope("bwd%d" % g):
@@ -361,6 +340,9 @@
                     ]))
                 own_part[g, s] = backward(s, me_z) + jnp.concatenate(lines, axis=1)
 
+    def forward(k, g, s, c):
+        return jnp.dot(ag[k, g, c, s], green_t[c, s], preferred_element_type=jnp.float32)
+
     def gather(k, g):
         with jax.named_scope("curv%d" % g):
             @pl.when(k > 0)
@@ -380,46 +362,29 @@
                 gradient = g_own[g, s] - step * fresh
                 g_own[g, s] = gradient
                 ag[k, g, me_z, s] = gradient.astype(jnp.bfloat16)
-                for peer in sent_to(g, s):
+                for peer in z_peers:
                     to_z(*gathered, k, g, peer, s).start()
                 square = square + jnp.sum(gradient * gradient, axis=1, keepdims=True)
-            relays(k, "g%d%d" % (g, s))
+            with jax.named_scope("fown%d" % g):
+                image = forward(k, g, s, me_z)
+                own_image[g] = image if s == 0 else own_image[g] + image
         with jax.named_scope("app%d" % g):
             nz_scalar[k, g, me_z] = jnp.broadcast_to(to_row(square), (8, LANES))
             for peer in z_peers:
                 to_z(*pix_sq, k, g, peer).start()
             apply_step(step, g)
 
-    def forward(k, g, s, c):
-        return lax.dot_general(
-            ag[k, g, c, s], green[c, s], (((1,), (1,)), ((), ())),
-            preferred_element_type=jnp.float32,
-        )
-
-    def forward_own(k, g):
-        with jax.named_scope("fown%d" % g):
-            image = forward(k, g, 0, me_z)
-            for s in range(1, SUB):
-                image = image + forward(k, g, s, me_z)
-            own_image[g] = image
-
     def forward_rest(k, g):
         image = own_image[g]
         with jax.named_scope("frest%d" % g):
-            seq = [(s, mask) for s in range(SUB) for mask in ((1, 2) if relayed(g, s) else (1, 3, 2))]
-            late = [(s, 3) for s in range(SUB) if relayed(g, s)]
-            cut = len(seq) - 3
-            seq = seq[:cut] + late[:1] + seq[cut:] + late[1:]
-            for i, (s, mask) in enumerate(seq):
-                source = flipped(me_z, mask, nz)
-                if not (relayed(g, s) and mask == 2):
-                    from_z(*gathered, k, g, source, s).wait_recv()
-                if i + 1 == len(seq):
+            turns = [(s, source) for s in range(SUB) for source in z_from]
+            for i, (s, source) in enumerate(turns):
+                from_z(*gathered, k, g, source, s).wait_recv()
+                if i + 1 == len(turns):
                     for copy in halo_copies(k, g):
                         copy.start()
                 image = image + forward(k, g, s, source)
-                relays(k, "f%d%d" % (g, i))
-                if i == 2:
+                if i + 1 == len(z_from):
                     for source in z_from:
                         from_z(*pix_sq, k, g, source).wait_recv()
                     npar_scalar[k, g, me_p] = jnp.broadcast_to(z_row(nz_scalar, k, g), (8, LANES))
@@ -470,10 +435,8 @@
                 rs_copy(k, g, peer, s).wait_send()
             to_z(*pix_sq, k, g, peer).wait_send()
         for s in range(SUB):
-            for peer in sent_to(g, s):
+            for peer in z_peers:
                 to_z(*gathered, k, g, peer, s).wait_send()
-            if relayed(g, s):
-                relay_copy(k, g, s).wait_send()
         for copy in halo_copies(k, g):
             copy.wait_send()
         for peer in p_peers:
@@ -481,21 +444,14 @@
             to_par(*images, k, g, peer).wait_send()
         finish_curvature(k + 1, g)
 
+    scatter(0, 0, loading=True)
+    with jax.named_scope("transp"):
+        for s, c in order:
+            green_t[c, s] = green[c, s].T
+
     @pl.loop(0, ITERS)
     def _(k):
-        @pl.when(k > 0)
-        def _():
-            advance(k - 1, 0)
-
-        scatter(k, 0)
-
-        @pl.when(k > 0)
-        def _():
-            forward_rest(k - 1, 1)
-            finish_sends(k - 1, 0)
-
         gather(k, 0)
-        forward_own(k, 0)
 
         @pl.when(k > 0)
         def _():
@@ -509,12 +465,16 @@
 
         forward_rest(k, 0)
         gather(k, 1)
-        forward_own(k, 1)
-
-    advance(ITERS - 1, 0)
-    forward_rest(ITERS - 1, 1)
+        advance(k, 0)
+
+        @pl.when(k + 1 < ITERS)
+        def _():
+            scatter(k + 1, 0)
+
+        forward_rest(k, 1)
+        finish_sends(k, 0)
+
     with jax.named_scope("final"):
-        finish_sends(ITERS - 1, 0)
         wait_curvature(ITERS, 0)
         apply_step(to_column(step_row(ITERS, 0), size), 0)
     advance(ITERS - 1, 1)
@@ -566,6 +526,7 @@
         out_specs=(vmem, vmem),
         scratch_shapes=[
             pltpu.VMEM((nz, SUB, pixels, width), bf16),
+            pltpu.VMEM((nz, SUB, width, pixels), bf16),
             pltpu.VMEM((GROUPS, size, pixels), bf16),
             pltpu.VMEM((GROUPS, size, pixels), f32),
             pltpu.VMEM((GROUPS, size, pixels), f32),
@@ -586,7 +547,6 @@
             dma((nz, SUB)),
             dma((n, GROUPS, nz, SUB)), dma((n, GROUPS, nz, SUB)),
             dma((n, GROUPS, nz, SUB)), dma((n, GROUPS, nz, SUB)),
-            dma((n, GROUPS, nz, SUB)),
             dma((n, GROUPS, npar)), dma((n, GROUPS, npar)),
             dma((n, GROUPS, 2)), dma((n, GROUPS, 2)),
             dma((n + 1, GROUPS, nz)), dma((n + 1, GROUPS, nz)),

time: 106 us -> 101 us (0.953)
  Pallas kernels: 105 us -> 100 us
    pallas_call x1, Pallas kernels: 103 us -> 98.2 us  [on_device_kernel(): pl.pallas_call(functools.partial(cgls_kernel, nz, npar), out_shape=(jax.S...]
where the time goes in v2:
time: 101 us
  Pallas kernels  100 us (99%)
    pallas_call x1, Pallas kernels, on_device_kernel(): pl.pallas_call(functools.partial(cgls_kernel, nz, npar), out_shape=(jax.S...  98.2 us

profile of v2, /device:TPU:0, one launch (start us, length us, event | category | flops | bytes accessed | tf_op | source)
XLA Modules:
  0.0 100.7 jit_solution(12399651550714305305)
XLA Ops:
  0.6 98.2 %shard_map.41 = (f32[32,4096]{1,0:T(8,128)}, f32[32,1152]{1,0:T(8,128)}) custom-call(bf16[1152,4096]{1,0:T(8,128)(2,1)} %green_hbm.1, bf16[32,1152]{1,0:T(8,128)(2,1)} %obs_ref.1), custom_call_target="tpu_custom_call" | custom-call | tf_op jit(solution)/shard_map/pallas_call | solution.py:519
  98.8 1.9 %shard_map.42 = (f32[32,4096]{1,0:T(8,128)}, f32[32,1152]{1,0:T(8,128)}) custom-call(f32[32,4096]{1,0:T(8,128)} %get-tuple-element.4.x_ref, f32[32,1152]{1,0:T(8,128)} %get-tuple-element.5.r_ref), custom_call_target="tpu_custom_call" | custom-call | tf_op jit(solution)/shard_map/pallas_call | solution.py:501

commit v3 on v2

--- a/solution.py
+++ b/solution.py
@@ -12,6 +12,7 @@
 LANES = 128
 SUB = 2
 GROUPS = 2
+STOPS = (3, 6)
 
 
 def padded_2(block, sides, width):
@@ -134,11 +135,11 @@
 
 def cgls_kernel(
     nz, npar,
-    green_hbm, obs_ref, x_ref, r_ref,
-    green, green_t, imb, im, own_image, p_ext, sp, g_own, own_part, gg_ref,
+    green_hbm, obs_hbm, x_ref, r_ref,
+    obs_ref, green, green_t, imb, im, own_image, p_ext, sp, g_own, own_part, gg_ref,
     rs_send, rs_recv, ag, h_recv, halo,
     sz, sp_scalar, nz_scalar, npar_scalar,
-    load_sem, rs_ss, rs_rs, ag_ss, ag_rs, h_ss, h_rs, halo_ss, halo_rs,
+    obs_sem, load_sem, rs_ss, rs_rs, ag_ss, ag_rs, h_ss, h_rs, halo_ss, halo_rs,
     sz_ss, sz_rs, sp_ss, sp_rs, nz_ss, nz_rs, np_ss, np_rs,
 ):
     me_z = lax.axis_index("pix")
@@ -166,6 +167,8 @@
             green_hbm.at[:, pl.ds(first, width)], green.at[c, s], load_sem.at[c, s]
         )
 
+    obs_copy = pltpu.make_async_copy(obs_hbm, obs_ref, obs_sem)
+    obs_copy.start()
     for s, c in order:
         load(s, c).start()
 
@@ -175,10 +178,6 @@
     for j in range(1, npar):
         pl.semaphore_signal(barrier, inc=1, device_id={"par": lax.rem(me_p + j, npar)}, device_id_type=MESH)
 
-    for g in groups:
-        mine = slice(g * size, (g + 1) * size)
-        imb[g] = obs_ref[mine]
-        r_ref[mine] = obs_ref[mine].astype(jnp.float32)
     im[...] = jnp.zeros_like(im)
     p_ext[...] = jnp.zeros_like(p_ext)
     sp[...] = jnp.zeros_like(sp)
@@ -187,6 +186,11 @@
     g_own[...] = jnp.zeros_like(g_own)
     gg_ref[...] = jnp.zeros_like(gg_ref)
     x_ref[...] = jnp.zeros_like(x_ref)
+    obs_copy.wait()
+    for g in groups:
+        mine = slice(g * size, (g + 1) * size)
+        imb[g] = obs_ref[mine]
+        r_ref[mine] = obs_ref[mine].astype(jnp.float32)
 
     with jax.named_scope("barrier"):
         pl.semaphore_wait(barrier, nz + npar - 2)
@@ -231,15 +235,15 @@
         return value
 
     def z_row(buf, k, g):
-        return total_row([buf[k, g, i, 0:1] for i in range(nz)])
+        return total_row([buf[k, g, i] for i in range(nz)])
 
     def par_row(buf, k, g):
-        return total_row([buf[k, g, i, 0:1] for i in range(npar)])
+        return total_row([buf[k, g, i] for i in range(npar)])
 
     def send_image_sq(k, g):
         image = im[g]
         row = to_row(jnp.sum(image * image, axis=1, keepdims=True))
-        sz[k, g, me_z] = jnp.broadcast_to(row, (8, LANES))
+        sz[k, g, me_z] = row
         for peer in z_peers:
             to_z(*image_sq, k, g, peer).start()
 
@@ -259,7 +263,7 @@
                 square = square + line * line
             sp[g, :, i * GRID:(i + 1) * GRID] = line
         row = to_row(jnp.sum(square, axis=1, keepdims=True))
-        sp_scalar[k, g, me_p] = jnp.broadcast_to(row, (8, LANES))
+        sp_scalar[k, g, me_p] = row
         for peer in p_peers:
             to_par(*smooth_sq, k, g, peer).start()
 
@@ -270,7 +274,7 @@
             from_z(*image_sq, k, g, peer).wait_recv()
 
     def step_row(k, g):
-        return gg_ref[g, 0:1] / (z_row(sz, k, g) + par_row(sp_scalar, k, g))
+        return gg_ref[g] / (z_row(sz, k, g) + par_row(sp_scalar, k, g))
 
     def apply_step(step, g):
         mine = slice(g * size, (g + 1) * size)
@@ -325,10 +329,14 @@
             return jnp.dot(vector, green[c, s], preferred_element_type=jnp.float32)
 
         with jax.named_scope("bwd%d" % g):
-            for s in range(SUB):
-                for peer in z_peers:
-                    rs_send[k, g, peer, s] = backward(s, peer).astype(jnp.bfloat16)
-                    rs_copy(k, g, peer, s).start()
+            turns = [(s, peer) for s in range(SUB) for peer in z_peers]
+            ready = backward(*turns[0])
+            for i, (s, peer) in enumerate(turns):
+                value = ready
+                if i + 1 < len(turns):
+                    ready = backward(*turns[i + 1])
+                rs_send[k, g, peer, s] = value.astype(jnp.bfloat16)
+                rs_copy(k, g, peer, s).start()
         with jax.named_scope("own%d" % g):
             for s in range(SUB):
                 base = (me_z * SUB + s) * own_rows
@@ -369,7 +377,7 @@
                 image = forward(k, g, s, me_z)
                 own_image[g] = image if s == 0 else own_image[g] + image
         with jax.named_scope("app%d" % g):
-            nz_scalar[k, g, me_z] = jnp.broadcast_to(to_row(square), (8, LANES))
+            nz_scalar[k, g, me_z] = to_row(square)
             for peer in z_peers:
                 to_z(*pix_sq, k, g, peer).start()
             apply_step(step, g)
@@ -378,16 +386,19 @@
         image = own_image[g]
         with jax.named_scope("frest%d" % g):
             turns = [(s, source) for s in range(SUB) for source in z_from]
-            for i, (s, source) in enumerate(turns):
-                from_z(*gathered, k, g, source, s).wait_recv()
-                if i + 1 == len(turns):
+            for i, stop in enumerate(STOPS):
+                batch = turns[STOPS[i - 1] if i else 0:stop]
+                for s, source in batch:
+                    from_z(*gathered, k, g, source, s).wait_recv()
+                if i + 1 == len(STOPS):
                     for copy in halo_copies(k, g):
                         copy.start()
-                image = image + forward(k, g, s, source)
-                if i + 1 == len(z_from):
+                for s, source in batch:
+                    image = image + forward(k, g, s, source)
+                if i == 0:
                     for source in z_from:
                         from_z(*pix_sq, k, g, source).wait_recv()
-                    npar_scalar[k, g, me_p] = jnp.broadcast_to(z_row(nz_scalar, k, g), (8, LANES))
+                    npar_scalar[k, g, me_p] = z_row(nz_scalar, k, g)
                     for peer in p_peers:
                         to_par(*par_sq, k, g, peer).start()
         with jax.named_scope("hsend%d" % g):
@@ -403,8 +414,8 @@
                 copy.wait_recv()
         with jax.named_scope("pupd%d" % g):
             fresh_sq = par_row(npar_scalar, k, g)
-            ratio = to_column(jnp.where(k == 0, 0.0, fresh_sq / gg_ref[g, 0:1]), size)
-            gg_ref[g] = jnp.broadcast_to(fresh_sq, (8, LANES))
+            ratio = to_column(jnp.where(k == 0, 0.0, fresh_sq / gg_ref[g]), size)
+            gg_ref[g] = fresh_sq
             for c in range(nz):
                 for s in range(SUB):
                     first = edge + (c * SUB + s) * width
@@ -522,9 +533,10 @@
             jax.ShapeDtypeStruct((sets, cells), f32),
             jax.ShapeDtypeStruct((sets, pixels), f32),
         ),
-        in_specs=[pl.BlockSpec(memory_space=pl.ANY), vmem],
+        in_specs=[pl.BlockSpec(memory_space=pl.ANY), pl.BlockSpec(memory_space=pl.ANY)],
         out_specs=(vmem, vmem),
         scratch_shapes=[
+            pltpu.VMEM((sets, pixels), bf16),
             pltpu.VMEM((nz, SUB, pixels, width), bf16),
             pltpu.VMEM((nz, SUB, width, pixels), bf16),
             pltpu.VMEM((GROUPS, size, pixels), bf16),
@@ -534,16 +546,17 @@
             pltpu.VMEM((GROUPS, size, cells + 2 * GRID), f32),
             pltpu.VMEM((GROUPS, SUB, size, width), f32),
             pltpu.VMEM((GROUPS, SUB, size, width), f32),
-            pltpu.VMEM((GROUPS, 8, LANES), f32),
+            pltpu.VMEM((GROUPS, 1, LANES), f32),
             pltpu.VMEM((n, GROUPS, nz, SUB, size, width), bf16),
             pltpu.VMEM((n, GROUPS, nz, SUB, size, width), bf16),
             pltpu.VMEM((n, GROUPS, nz, SUB, size, width), bf16),
             pltpu.VMEM((n, GROUPS, npar, size, pixels), bf16),
             pltpu.VMEM((n, GROUPS, 2, size, 2 * GRID), bf16),
-            pltpu.VMEM((n + 1, GROUPS, nz, 8, LANES), f32),
-            pltpu.VMEM((n + 1, GROUPS, npar, 8, LANES), f32),
-            pltpu.VMEM((n, GROUPS, nz, 8, LANES), f32),
-            pltpu.VMEM((n, GROUPS, npar, 8, LANES), f32),
+            pltpu.VMEM((n + 1, GROUPS, nz, 1, LANES), f32),
+            pltpu.VMEM((n + 1, GROUPS, npar, 1, LANES), f32),
+            pltpu.VMEM((n, GROUPS, nz, 1, LANES), f32),
+            pltpu.VMEM((n, GROUPS, npar, 1, LANES), f32),
+            dma,
             dma((nz, SUB)),
             dma((n, GROUPS, nz, SUB)), dma((n, GROUPS, nz, SUB)),
             dma((n, GROUPS, nz, SUB)), dma((n, GROUPS, nz, SUB)),

time: 101 us -> 94.4 us (0.935)
  Pallas kernels: 100 us -> 93.6 us
    pallas_call x1, Pallas kernels: 98.2 us -> 91.6 us  [on_device_kernel(): pl.pallas_call(functools.partial(cgls_kernel, nz, npar), out_shape=(jax.S...]
where the time goes in v3:
time: 94.4 us; the launch traced here: 94.2 us
  Pallas kernels  93.6 us (99%)
    pallas_call x1, Pallas kernels, on_device_kernel(): pl.pallas_call(functools.partial(cgls_kernel, nz, npar), out_shape=(jax.S...  91.6 us
    pallas_call x1, Pallas kernels, finish(): pl.pallas_call(finish_kernel, out_shape=(jax.ShapeDtypeStruct(x.shape, x....  1.92 us

profile of v3, /device:TPU:0, one launch (start us, length us, event | category | flops | bytes accessed | tf_op | source)
XLA Modules:
  0.0 94.2 jit_solution(7848557801709439414)
XLA Ops:
  0.6 91.6 %shard_map.41 = (f32[32,4096]{1,0:T(8,128)}, f32[32,1152]{1,0:T(8,128)}) custom-call(bf16[1152,4096]{1,0:T(8,128)(2,1)} %green_hbm.1, bf16[32,1152]{1,0:T(8,128)(2,1)} %obs_hbm.1), custom_call_target="tpu_custom_call" | custom-call | tf_op jit(solution)/shard_map/pallas_call | solution.py:530
  92.3 1.9 %shard_map.42 = (f32[32,4096]{1,0:T(8,128)}, f32[32,1152]{1,0:T(8,128)}) custom-call(f32[32,4096]{1,0:T(8,128)} %get-tuple-element.4.x_ref, f32[32,1152]{1,0:T(8,128)} %get-tuple-element.5.r_ref), custom_call_target="tpu_custom_call" | custom-call | tf_op jit(solution)/shard_map/pallas_call | solution.py:512

commit v4 on v3

--- a/solution.py
+++ b/solution.py
@@ -373,9 +373,11 @@
                 for peer in z_peers:
                     to_z(*gathered, k, g, peer, s).start()
                 square = square + jnp.sum(gradient * gradient, axis=1, keepdims=True)
-            with jax.named_scope("fown%d" % g):
-                image = forward(k, g, s, me_z)
-                own_image[g] = image if s == 0 else own_image[g] + image
+        with jax.named_scope("fown%d" % g):
+            image = forward(k, g, 0, me_z)
+            for s in range(1, SUB):
+                image = image + forward(k, g, s, me_z)
+            own_image[g] = image
         with jax.named_scope("app%d" % g):
             nz_scalar[k, g, me_z] = to_row(square)
             for peer in z_peers:

time: 94.4 us -> 94.2 us (level)
  no operation moved by 1% of the time
where the time goes in v4:
time: 94.2 us; the launch traced here: 94.1 us
  Pallas kernels  93.4 us (99%)
    pallas_call x1, Pallas kernels, on_device_kernel(): pl.pallas_call(functools.partial(cgls_kernel, nz, npar), out_shape=(jax.S...  91.5 us
    pallas_call x1, Pallas kernels, finish(): pl.pallas_call(finish_kernel, out_shape=(jax.ShapeDtypeStruct(x.shape, x....  1.92 us

profile of v4, /device:TPU:0, one launch (start us, length us, event | category | flops | bytes accessed | tf_op | source)
XLA Modules:
  0.0 94.1 jit_solution(17767313321111878164)
XLA Ops:
  0.6 91.5 %shard_map.41 = (f32[32,4096]{1,0:T(8,128)}, f32[32,1152]{1,0:T(8,128)}) custom-call(bf16[1152,4096]{1,0:T(8,128)(2,1)} %green_hbm.1, bf16[32,1152]{1,0:T(8,128)(2,1)} %obs_hbm.1), custom_call_target="tpu_custom_call" | custom-call | tf_op jit(solution)/shard_map/pallas_call | solution.py:532
  92.2 1.9 %shard_map.42 = (f32[32,4096]{1,0:T(8,128)}, f32[32,1152]{1,0:T(8,128)}) custom-call(f32[32,4096]{1,0:T(8,128)} %get-tuple-element.4.x_ref, f32[32,1152]{1,0:T(8,128)} %get-tuple-element.5.r_ref), custom_call_target="tpu_custom_call" | custom-call | tf_op jit(solution)/shard_map/pallas_call | solution.py:514
